TPU v7x, 256 devices: a whole 4x4x8 slice. The times are simulated.
256 devices in a mesh: row: 8 (over z), col: 16 (over y_lo, x, core), layer: 2 (over y_hi).
Axes of the slice: x: 4, y: 4 (y_hi: 2, y_lo: 2; y = y_hi * 2 + y_lo), z: 8, core: 2. Of those that a mesh axis runs over, the one named last changes fastest.
Arguments:
- left: bfloat16 [8192, 8192], P('row', ('col', 'layer')), may hold values from -6 to 6
- middle: bfloat16 [8192, 8192], P('row', 'col'), may hold values from -0.0625 to 0.0625
- right: bfloat16 [8192, 8192], P('row', 'col'), may hold values from -0.0625 to 0.0625
Outputs:
- product: bfloat16 [8192, 8192], P('row', ('col', 'layer'))
All inputs are finite; a program needn't handle non-finite values.
Results may differ from a plain program's by a relative error of at most 0.0049.
Values may be sent and summed in bfloat16 or wider, within the bound.
A program may use at most 64 MiB of HBM per device.

v0:
```python
import jax
import jax.numpy as jnp
from jax import lax
from jax.sharding import PartitionSpec as P


def split_up(array, dim, size):
    lengths = array.shape
    blocks = array.reshape(*lengths[:dim], size, lengths[dim] // size, *lengths[dim + 1 :])
    return jnp.moveaxis(blocks, dim, 0)


def sum_at_owner(array, axis, dim):
    blocks = split_up(array, dim, lax.axis_size(axis))
    arrived = lax.all_to_all(blocks, axis, split_axis=0, concat_axis=0, tiled=True)
    return arrived.sum(axis=0)


def multiply(left, right):
    width = left.shape[1]
    layers = lax.axis_size("layer")
    layer_index = lax.axis_index("layer")
    columns = right.shape[1]
    groups = right.shape[0] // width // layers
    shaped = right.reshape(groups, layers, width, columns)
    own_rows = lax.dynamic_index_in_dim(shaped, layer_index, 1, keepdims=False).reshape(
        groups * width, columns
    )
    right_all = lax.all_gather(own_rows, "row", axis=0, tiled=True)
    return jnp.dot(
        lax.all_gather(left, "col", axis=1, tiled=True),
        right_all,
        preferred_element_type=jnp.float32,
    )


def per_device(left, middle, right):
    partial_value = multiply(left, middle)
    first = sum_at_owner(partial_value, "layer", 1)
    first = first.astype(jnp.bfloat16)
    second = multiply(first, right)
    return sum_at_owner(second, "layer", 1).astype(jnp.bfloat16)


def solution(mesh):
    return jax.shard_map(
        per_device,
        mesh=mesh,
        in_specs=(P("row", ("col", "layer")), P("row", "col"), P("row", "col")),
        out_specs=P("row", ("col", "layer")),
        check_vma=False,
    )
```

profile of v0, /device:TPU:1, one launch (start us, length us, event | category | flops | bytes accessed | tf_op | source)
XLA Modules:
  0.0 290.7 jit_solution(16866077000397679622)
XLA Ops:
  6.5 0.0 copy-start
  6.5 0.0 all-gather.5.cloned.1.call-start
  6.5 1.2 copy-done
  7.8 0.8 constant_dynamic-slice_fusion.1
  8.6 0.0 all-gather.5.cloned.1.call-update
  8.6 0.0 all-gather.7.cloned.1.call-start
  8.7 0.7 all-gather.7.cloned.1.call-update
  9.4 0.0 all-gather.11.cloned.1.call-start
  9.4 1.9 constant_dynamic-slice_fusion
  11.3 0.0 all-gather.11.cloned.1.call-update
  11.3 0.0 all-gather.9.cloned.1.call-start
  11.4 56.2 %all-gather.5.cloned.1.call-done = bf16[4096,512]{1,0:T(8,128)(2,1)} async-done(((bf16[512,512]{1,0:T(8,128)(2,1)}), bf16[4096,512]{1,0:T(8,128)(2,1)}) %all-gather.5.cloned.1.call-update) | async-done | bytes 4194320 | tf_op jit(solution)/shard_map/all_gather | solution.py:29
  67.5 64.4 %all-gather.7.cloned.1.call-done = bf16[1024,4096]{1,0:T(8,128)(2,1)} async-done(((bf16[1024,256]{1,0:T(8,128)(2,1)}), bf16[1024,4096]{1,0:T(8,128)(2,1)}) %all-gather.7.cloned.1.call-update) | async-done | bytes 8388624 | tf_op jit(solution)/shard_map/all_gather | solution.py:31
  131.9 8.2 %fusion = f32[512,1024]{1,0:T(8,128)S(1)} fusion(bf16[4096,512]{1,0:T(8,128)(2,1)} %all-gather.5.cloned.1.call-done, bf16[1024,4096]{1,0:T(8,128)(2,1)} %all-gather.7.cloned.1.call-done), kind=kOutput, calls=%fused_computation.2 | convolution fusion | flops 4294967296 | bytes 14680064 | tf_op jit(solution)/shard_map/dot_general | solution.py:30
  140.1 28.8 %all_to_all.10 = f32[2,1024,256]{1,2,0:T(8,128)S(1)} all-to-all(f32[2,1024,256]{1,2,0:T(8,128)S(1)} %bitcast.17), channel_id=1, replica_groups=mesh['row'=8,'col'=16,'layer'=2] {'layer'}, dimensions={0} | all-to-all | bytes 4194304 | tf_op jit(solution)/shard_map/all_to_all | solution.py:15
  168.9 1.1 reduce_sum.18
  170.0 0.0 all-gather.9.cloned.1.call-update
  170.0 17.7 %all-gather.11.cloned.1.call-done = bf16[4096,512]{1,0:T(8,128)(2,1)} async-done(((bf16[512,512]{1,0:T(8,128)(2,1)}), bf16[4096,512]{1,0:T(8,128)(2,1)}) %all-gather.11.cloned.1.call-update) | async-done | bytes 4194320 | tf_op jit(solution)/shard_map/all_gather | solution.py:29
  187.7 55.5 %all-gather.9.cloned.1.call-done = bf16[1024,4096]{0,1:T(8,128)(2,1)} async-done(((bf16[1024,256]{0,1:T(8,128)(2,1)}), bf16[1024,4096]{0,1:T(8,128)(2,1)}) %all-gather.9.cloned.1.call-update) | async-done | bytes 8388624 | tf_op jit(solution)/shard_map/all_gather | solution.py:31
  243.2 8.2 %fusion.1 = f32[1024,512]{0,1:T(8,128)S(1)} fusion(bf16[1024,4096]{0,1:T(8,128)(2,1)} %all-gather.9.cloned.1.call-done, bf16[4096,512]{1,0:T(8,128)(2,1)} %all-gather.11.cloned.1.call-done), kind=kOutput, calls=%fused_computation.3 | convolution fusion | flops 4294967296 | bytes 14680064 | tf_op jit(solution)/shard_map/dot_general | solution.py:30
  251.4 29.6 %all_to_all.11 = f32[2,1024,256]{1,2,0:T(8,128)S(1)} all-to-all(f32[2,1024,256]{1,2,0:T(8,128)S(1)} %bitcast.18), channel_id=1, replica_groups=mesh['row'=8,'col'=16,'layer'=2] {'layer'}, dimensions={0} | all-to-all | bytes 4194304 | tf_op jit(solution)/shard_map/all_to_all | solution.py:15
  281.0 1.1 reduce_sum.19
  282.1 2.0 copy.4
Async XLA Ops:
  6.5 1.2 copy-start
  6.5 61.0 %all-gather.5.cloned.1.call-start = ((), (), s32[]{:S(2)}) async-start(), calls=%async_computation.2 | async-start | bytes 4718592 | tf_op jit(solution)/shard_map/all_gather | solution.py:29
  8.6 123.3 %all-gather.7.cloned.1.call-start = ((), (), s32[]{:S(2)}) async-start(), calls=%async_computation.3 | async-start | bytes 8912896 | tf_op jit(solution)/shard_map/all_gather | solution.py:31
  9.4 178.3 %all-gather.11.cloned.1.call-start = ((), (), s32[]{:S(2)}) async-start(), calls=%async_computation.5 | async-start | bytes 4718592 | tf_op jit(solution)/shard_map/all_gather | solution.py:29
  11.3 231.9 %all-gather.9.cloned.1.call-start = ((), (), s32[]{:S(2)}) async-start(), calls=%async_computation.4 | async-start | bytes 8912896 | tf_op jit(solution)/shard_map/all_gather | solution.py:31
Sparse Core Ops, SparseCore 0:
  9.1 58.3 all-gather.4
  69.3 62.5 all-gather.6
  133.7 53.9 all-gather.10
  189.4 53.7 all-gather.8
where the time goes:
time: 291 us
  waiting for transfers between devices  194 us (67%)
  blocking collectives  58.3 us (20%)
  matrix products  16.5 us (6%)
  between operations  13.1 us (5%)
  local copies, waits for them, and re-layouts  5.97 us (2%)
    all_gather x2, waiting for transfers between devices, multiply(): lax.all_gather(left, 'col', axis=1, tiled=True)  120 us
    all_gather x2, waiting for transfers between devices, multiply(): right_all = lax.all_gather(own_rows, 'row', axis=0, tiled=True)  73.8 us
    all_to_all x2, blocking collectives, sum_at_owner(): lax.all_to_all(blocks, axis, split_axis=0, concat_axis=0, tiled=True)  58.3 us
    dot_general x2, matrix products, multiply(): jnp.dot(lax.all_gather(left, 'col', axis=1, tiled=True), right_all, prefe...  16.5 us
  transfers between devices with their start and end apart: 4, of which 4 were waited for; matrix products, arithmetic and copies ran while one was open for 4% of the time, Pallas kernels for 0%

commit v1 on v0

--- a/solution.py
+++ b/solution.py
@@ -2,6 +2,23 @@
 import jax.numpy as jnp
 from jax import lax
 from jax.sharding import PartitionSpec as P
+
+
+def in_order(parts, dim):
+    shape = list(parts.shape[1:])
+    shape[dim] *= parts.shape[0]
+    return jnp.moveaxis(parts, 0, dim).reshape(shape)
+
+
+def gather_around(array, axis, dim):
+    size = lax.axis_size(axis)
+    ahead = [(i, (i + 1) % size) for i in range(size)]
+    blocks = [array]
+    while len(blocks) < size:
+        blocks.append(lax.ppermute(blocks[-1], axis, ahead))
+    index = lax.axis_index(axis)
+    blocks = jnp.stack(blocks)[(index - jnp.arange(size)) % size]
+    return in_order(blocks, dim)
 
 
 def split_up(array, dim, size):
@@ -26,7 +43,7 @@
     own_rows = lax.dynamic_index_in_dim(shaped, layer_index, 1, keepdims=False).reshape(
         groups * width, columns
     )
-    right_all = lax.all_gather(own_rows, "row", axis=0, tiled=True)
+    right_all = gather_around(own_rows, "row", 0)
     return jnp.dot(
         lax.all_gather(left, "col", axis=1, tiled=True),
         right_all,

time: 291 us -> 288 us (0.990)
  the two profiles are of different devices: /device:TPU:1 before, /device:TPU:4 now
where the time goes in v1:
time: 288 us; the launch traced here: 287 us
  waiting for transfers between devices  174 us (60%)
  blocking collectives  43.7 us (15%)
  local copies, waits for them, and re-layouts  35.6 us (12%)
  matrix products  16.4 us (6%)
  between operations  13.5 us (5%)
    ppermute x14, waiting for transfers between devices, gather_around(): blocks.append(lax.ppermute(blocks[-1], axis, ahead))  173 us
    all_to_all x2, blocking collectives, sum_at_owner(): lax.all_to_all(blocks, axis, split_axis=0, concat_axis=0, tiled=True)  43.7 us
    dot_general x2, matrix products, multiply(): jnp.dot(lax.all_gather(left, 'col', axis=1, tiled=True), right_all, prefe...  16.4 us
    unnamed x18, local copies, waits for them, and re-layouts  14.4 us
    gather x2, local copies, waits for them, and re-layouts, gather_around(): blocks = jnp.stack(blocks)[(index - jnp.arange(size)) % size]  9.91 us
    dot_general x1, local copies, waits for them, and re-layouts, multiply(): jnp.dot(lax.all_gather(left, 'col', axis=1, tiled=True), right_all, prefe...  6.44 us
  transfers between devices with their start and end apart: 16, of which 14 were waited for; matrix products, arithmetic and copies ran while one was open for 12% of the time, Pallas kernels for 0%

profile of v1, /device:TPU:4, one launch (start us, length us, event | category | flops | bytes accessed | tf_op | source)
XLA Modules:
  0.0 287.0 jit_solution(18411777771239815482)
XLA Ops:
  7.8 2.0 collective-permute-start
  9.8 15.9 %collective-permute-done = bf16[512,512]{1,0:T(8,128)(2,1)S(1)} collective-permute-done((bf16[512,512]{1,0:T(8,128)(2,1)S(1)}, bf16[512,512]{1,0:T(8,128)(2,1)S(1)}, u32[]{:S(2)}, u32[]{:S(2)}) %collective-permute-start) | collective-permute-done | bytes 524320 | tf_op jit(solution)/shard_map/ppermute | solution.py:18
  25.7 14.3 %collective-permute-done.1 = bf16[512,512]{1,0:T(8,128)(2,1)S(1)} collective-permute-done((bf16[512,512]{1,0:T(8,128)(2,1)S(1)}, bf16[512,512]{1,0:T(8,128)(2,1)S(1)}, u32[]{:S(2)}, u32[]{:S(2)}) %collective-permute-start.1) | collective-permute-done | bytes 524320 | tf_op jit(solution)/shard_map/ppermute | solution.py:18
  40.0 13.4 %collective-permute-done.2 = bf16[512,512]{1,0:T(8,128)(2,1)S(1)} collective-permute-done((bf16[512,512]{1,0:T(8,128)(2,1)S(1)}, bf16[512,512]{1,0:T(8,128)(2,1)S(1)}, u32[]{:S(2)}, u32[]{:S(2)}) %collective-permute-start.2) | collective-permute-done | bytes 524320 | tf_op jit(solution)/shard_map/ppermute | solution.py:18
  53.4 12.6 %collective-permute-done.3 = bf16[512,512]{1,0:T(8,128)(2,1)S(1)} collective-permute-done((bf16[512,512]{1,0:T(8,128)(2,1)S(1)}, bf16[512,512]{1,0:T(8,128)(2,1)S(1)}, u32[]{:S(2)}, u32[]{:S(2)}) %collective-permute-start.3) | collective-permute-done | bytes 524320 | tf_op jit(solution)/shard_map/ppermute | solution.py:18
  66.9 11.0 %collective-permute-done.4 = bf16[512,512]{1,0:T(8,128)(2,1)} collective-permute-done((bf16[512,512]{1,0:T(8,128)(2,1)S(1)}, bf16[512,512]{1,0:T(8,128)(2,1)}, u32[]{:S(2)}, u32[]{:S(2)}) %collective-permute-start.4) | collective-permute-done | bytes 524320 | tf_op jit(solution)/shard_map/ppermute | solution.py:18
  81.4 8.8 %collective-permute-done.5 = bf16[512,512]{1,0:T(8,128)(2,1)S(1)} collective-permute-done((bf16[512,512]{1,0:T(8,128)(2,1)}, bf16[512,512]{1,0:T(8,128)(2,1)S(1)}, u32[]{:S(2)}, u32[]{:S(2)}) %collective-permute-start.5) | collective-permute-done | bytes 524320 | tf_op jit(solution)/shard_map/ppermute | solution.py:18
  91.0 1.9 bitcast_dynamic-update-slice_fusion.9
  93.7 6.8 %collective-permute-done.6 = bf16[512,512]{1,0:T(8,128)(2,1)S(1)} collective-permute-done((bf16[512,512]{1,0:T(8,128)(2,1)S(1)}, bf16[512,512]{1,0:T(8,128)(2,1)S(1)}, u32[]{:S(2)}, u32[]{:S(2)}) %collective-permute-start.6) | collective-permute-done | bytes 524320 | tf_op jit(solution)/shard_map/ppermute | solution.py:18
  101.4 5.0 %gather_fusion = bf16[8,512,512]{2,1,0:T(8,128)(2,1)} fusion(bf16[8,512,512]{2,1,0:T(8,128)(2,1)} %bitcast_dynamic-update-slice_fusion.7, s32[1024]{0:T(1024)S(1)} %pad_clamp_fusion), kind=kCustom, calls=%fused_computation | custom fusion | bytes 8388640 | tf_op jit(solution)/shard_map/gather | solution.py:20
  106.4 8.2 %fusion.7 = f32[512,1024]{1,0:T(8,128)S(1)} fusion(bf16[4096,512]{1,0:T(8,128)(2,1)} %bitcast.62, bf16[1024,4096]{1,0:T(8,128)(2,1)} %all-gather.3.cloned.1.call-done), kind=kOutput, calls=%fused_computation.30 | convolution fusion | flops 4294967296 | bytes 14680064 | tf_op jit(solution)/shard_map/dot_general | solution.py:47
  114.6 24.6 %all_to_all.10 = f32[2,1024,256]{1,2,0:T(8,128)S(1)} all-to-all(f32[2,1024,256]{1,2,0:T(8,128)S(1)} %bitcast.63), channel_id=1, replica_groups=mesh['row'=8,'col'=16,'layer'=2] {'layer'}, dimensions={0} | all-to-all | bytes 4194304 | tf_op jit(solution)/shard_map/all_to_all | solution.py:32
  140.3 2.0 copy.6
  143.6 15.0 %collective-permute-done.7 = bf16[512,512]{1,0:T(8,128)(2,1)S(1)} collective-permute-done((bf16[512,512]{1,0:T(8,128)(2,1)S(1)}, bf16[512,512]{1,0:T(8,128)(2,1)S(1)}, u32[]{:S(2)}, u32[]{:S(2)}) %collective-permute-start.7) | collective-permute-done | bytes 524320 | tf_op jit(solution)/shard_map/ppermute | solution.py:18
  158.6 15.8 %collective-permute-done.8 = bf16[512,512]{1,0:T(8,128)(2,1)S(1)} collective-permute-done((bf16[512,512]{1,0:T(8,128)(2,1)S(1)}, bf16[512,512]{1,0:T(8,128)(2,1)S(1)}, u32[]{:S(2)}, u32[]{:S(2)}) %collective-permute-start.8) | collective-permute-done | bytes 524320 | tf_op jit(solution)/shard_map/ppermute | solution.py:18
  174.4 15.0 %collective-permute-done.9 = bf16[512,512]{1,0:T(8,128)(2,1)S(1)} collective-permute-done((bf16[512,512]{1,0:T(8,128)(2,1)S(1)}, bf16[512,512]{1,0:T(8,128)(2,1)S(1)}, u32[]{:S(2)}, u32[]{:S(2)}) %collective-permute-start.9) | collective-permute-done | bytes 524320 | tf_op jit(solution)/shard_map/ppermute | solution.py:18
  189.4 14.1 %collective-permute-done.10 = bf16[512,512]{1,0:T(8,128)(2,1)S(1)} collective-permute-done((bf16[512,512]{1,0:T(8,128)(2,1)S(1)}, bf16[512,512]{1,0:T(8,128)(2,1)S(1)}, u32[]{:S(2)}, u32[]{:S(2)}) %collective-permute-start.10) | collective-permute-done | bytes 524320 | tf_op jit(solution)/shard_map/ppermute | solution.py:18
  204.4 12.4 %collective-permute-done.11 = bf16[512,512]{1,0:T(8,128)(2,1)S(1)} collective-permute-done((bf16[512,512]{1,0:T(8,128)(2,1)S(1)}, bf16[512,512]{1,0:T(8,128)(2,1)S(1)}, u32[]{:S(2)}, u32[]{:S(2)}) %collective-permute-start.11) | collective-permute-done | bytes 524320 | tf_op jit(solution)/shard_map/ppermute | solution.py:18
  219.4 9.8 %collective-permute-done.12 = bf16[512,512]{1,0:T(8,128)(2,1)S(1)} collective-permute-done((bf16[512,512]{1,0:T(8,128)(2,1)S(1)}, bf16[512,512]{1,0:T(8,128)(2,1)S(1)}, u32[]{:S(2)}, u32[]{:S(2)}) %collective-permute-start.12) | collective-permute-done | bytes 524320 | tf_op jit(solution)/shard_map/ppermute | solution.py:18
  231.7 7.9 %collective-permute-done.13 = bf16[512,512]{1,0:T(8,128)(2,1)S(1)} collective-permute-done((bf16[512,512]{1,0:T(8,128)(2,1)S(1)}, bf16[512,512]{1,0:T(8,128)(2,1)S(1)}, u32[]{:S(2)}, u32[]{:S(2)}) %collective-permute-start.13) | collective-permute-done | bytes 524320 | tf_op jit(solution)/shard_map/ppermute | solution.py:18
  240.4 4.9 %gather_fusion.1 = bf16[8,512,512]{2,1,0:T(8,128)(2,1)} fusion(bf16[8,512,512]{2,1,0:T(8,128)(2,1)} %bitcast_dynamic-update-slice_fusion, s32[1024]{0:T(1024)S(1)} %pad_clamp_fusion), kind=kCustom, calls=%fused_computation.1 | custom fusion | bytes 8388640 | tf_op jit(solution)/shard_map/gather | solution.py:20
  245.4 6.4 %copy.8 = bf16[512,4096]{1,0:T(8,128)(2,1)} copy(bf16[512,4096]{0,1:T(8,128)(2,1)} %bitcast.60) | data formatting | bytes 8388608 | tf_op jit(solution)/shard_map/dot_general | solution.py:47
  251.8 8.2 %fusion.2 = f32[2,1024,256]{2,1,0:T(8,128)S(1)} fusion(bf16[2,256,4096]{2,1,0:T(8,128)(2,1)} %bitcast.61, bf16[1024,4096]{1,0:T(8,128)(2,1)} %all-gather.5.cloned.1.call-done), kind=kOutput, calls=%fused_computation.4 | convolution fusion | flops 4294967296 | bytes 14680064 | tf_op jit(solution)/shard_map/dot_general | solution.py:47
  260.0 19.1 %all_to_all.11 = f32[2,1024,256]{2,1,0:T(8,128)S(1)} all-to-all(f32[2,1024,256]{2,1,0:T(8,128)S(1)} %fusion.2), channel_id=1, replica_groups=mesh['row'=8,'col'=16,'layer'=2] {'layer'}, dimensions={0} | all-to-all | bytes 4194304 | tf_op jit(solution)/shard_map/all_to_all | solution.py:32
  (44 shorter events, 18.4 us)
Async XLA Ops:
  6.5 1.2 copy-start
  6.5 99.9 %all-gather.3.cloned.1.call-start = ((), (), s32[]{:S(2)}) async-start(), calls=%async_computation.2 | async-start | bytes 8912896 | tf_op jit(solution)/shard_map/all_gather | solution.py:48
  7.3 244.6 %all-gather.5.cloned.1.call-start = ((), (), s32[]{:S(2)}) async-start(), calls=%async_computation.3 | async-start | bytes 8912896 | tf_op jit(solution)/shard_map/all_gather | solution.py:48
  7.8 17.9 %collective-permute-start = (bf16[512,512]{1,0:T(8,128)(2,1)S(1)}, bf16[512,512]{1,0:T(8,128)(2,1)S(1)}, u32[]{:S(2)}, u32[]{:S(2)}) collective-permute-start(bf16[512,512]{1,0:T(8,128)(2,1)S(1)} %bitcast.64), channel_id=1, source_target_pairs={{0,32},{32,64},{64,96},{96,128},{128,160},{160,192},{192,224},{224... | collective-permute-start | bytes 1572872 | tf_op jit(solution)/shard_map/ppermute | solution.py:18
  25.7 14.3 %collective-permute-start.1 = (bf16[512,512]{1,0:T(8,128)(2,1)S(1)}, bf16[512,512]{1,0:T(8,128)(2,1)S(1)}, u32[]{:S(2)}, u32[]{:S(2)}) collective-permute-start(bf16[512,512]{1,0:T(8,128)(2,1)S(1)} %collective-permute-done), channel_id=1, source_target_pairs={{0,32},{32,64},{64,96},{96,128},{128,160},{160,192},{192,224},{224... | collective-permute-start | bytes 1572872 | tf_op jit(solution)/shard_map/ppermute | solution.py:18
  40.0 13.4 %collective-permute-start.2 = (bf16[512,512]{1,0:T(8,128)(2,1)S(1)}, bf16[512,512]{1,0:T(8,128)(2,1)S(1)}, u32[]{:S(2)}, u32[]{:S(2)}) collective-permute-start(bf16[512,512]{1,0:T(8,128)(2,1)S(1)} %collective-permute-done.1), channel_id=1, source_target_pairs={{0,32},{32,64},{64,96},{96,128},{128,160},{160,192},{192,224},{224... | collective-permute-start | bytes 1572872 | tf_op jit(solution)/shard_map/ppermute | solution.py:18
  53.4 12.6 %copy-start.1 = (bf16[512,512]{1,0:T(8,128)(2,1)}, bf16[512,512]{1,0:T(8,128)(2,1)S(1)}, u32[]{:S(2)}) copy-start(bf16[512,512]{1,0:T(8,128)(2,1)S(1)} %collective-permute-done.2) | copy-start | bytes 1572868
  53.4 12.6 %collective-permute-start.3 = (bf16[512,512]{1,0:T(8,128)(2,1)S(1)}, bf16[512,512]{1,0:T(8,128)(2,1)S(1)}, u32[]{:S(2)}, u32[]{:S(2)}) collective-permute-start(bf16[512,512]{1,0:T(8,128)(2,1)S(1)} %collective-permute-done.2), channel_id=1, source_target_pairs={{0,32},{32,64},{64,96},{96,128},{128,160},{160,192},{192,224},{224... | collective-permute-start | bytes 1572872 | tf_op jit(solution)/shard_map/ppermute | solution.py:18
  66.0 11.9 %collective-permute-start.4 = (bf16[512,512]{1,0:T(8,128)(2,1)S(1)}, bf16[512,512]{1,0:T(8,128)(2,1)}, u32[]{:S(2)}, u32[]{:S(2)}) collective-permute-start(bf16[512,512]{1,0:T(8,128)(2,1)S(1)} %collective-permute-done.3), channel_id=1, source_target_pairs={{0,32},{32,64},{64,96},{96,128},{128,160},{160,192},{192,224},{224... | collective-permute-start | bytes 1572872 | tf_op jit(solution)/shard_map/ppermute | solution.py:18
  77.9 12.3 %collective-permute-start.5 = (bf16[512,512]{1,0:T(8,128)(2,1)}, bf16[512,512]{1,0:T(8,128)(2,1)S(1)}, u32[]{:S(2)}, u32[]{:S(2)}) collective-permute-start(bf16[512,512]{1,0:T(8,128)(2,1)} %collective-permute-done.4), channel_id=1, source_target_pairs={{0,32},{32,64},{64,96},{96,128},{128,160},{160,192},{192,224},{224... | collective-permute-start | bytes 1572872 | tf_op jit(solution)/shard_map/ppermute | solution.py:18
  90.2 10.4 %collective-permute-start.6 = (bf16[512,512]{1,0:T(8,128)(2,1)S(1)}, bf16[512,512]{1,0:T(8,128)(2,1)S(1)}, u32[]{:S(2)}, u32[]{:S(2)}) collective-permute-start(bf16[512,512]{1,0:T(8,128)(2,1)S(1)} %collective-permute-done.5), channel_id=1, source_target_pairs={{0,32},{32,64},{64,96},{96,128},{128,160},{160,192},{192,224},{224... | collective-permute-start | bytes 1572872 | tf_op jit(solution)/shard_map/ppermute | solution.py:18
  143.5 15.1 %collective-permute-start.7 = (bf16[512,512]{1,0:T(8,128)(2,1)S(1)}, bf16[512,512]{1,0:T(8,128)(2,1)S(1)}, u32[]{:S(2)}, u32[]{:S(2)}) collective-permute-start(bf16[512,512]{1,0:T(8,128)(2,1)S(1)} %bitcast.66), channel_id=1, source_target_pairs={{0,32},{32,64},{64,96},{96,128},{128,160},{160,192},{192,224},{224... | collective-permute-start | bytes 1572872 | tf_op jit(solution)/shard_map/ppermute | solution.py:18
  158.6 15.8 %collective-permute-start.8 = (bf16[512,512]{1,0:T(8,128)(2,1)S(1)}, bf16[512,512]{1,0:T(8,128)(2,1)S(1)}, u32[]{:S(2)}, u32[]{:S(2)}) collective-permute-start(bf16[512,512]{1,0:T(8,128)(2,1)S(1)} %collective-permute-done.7), channel_id=1, source_target_pairs={{0,32},{32,64},{64,96},{96,128},{128,160},{160,192},{192,224},{224... | collective-permute-start | bytes 1572872 | tf_op jit(solution)/shard_map/ppermute | solution.py:18
  174.4 15.0 %collective-permute-start.9 = (bf16[512,512]{1,0:T(8,128)(2,1)S(1)}, bf16[512,512]{1,0:T(8,128)(2,1)S(1)}, u32[]{:S(2)}, u32[]{:S(2)}) collective-permute-start(bf16[512,512]{1,0:T(8,128)(2,1)S(1)} %collective-permute-done.8), channel_id=1, source_target_pairs={{0,32},{32,64},{64,96},{96,128},{128,160},{160,192},{192,224},{224... | collective-permute-start | bytes 1572872 | tf_op jit(solution)/shard_map/ppermute | solution.py:18
  189.4 14.1 %collective-permute-start.10 = (bf16[512,512]{1,0:T(8,128)(2,1)S(1)}, bf16[512,512]{1,0:T(8,128)(2,1)S(1)}, u32[]{:S(2)}, u32[]{:S(2)}) collective-permute-start(bf16[512,512]{1,0:T(8,128)(2,1)S(1)} %collective-permute-done.9), channel_id=1, source_target_pairs={{0,32},{32,64},{64,96},{96,128},{128,160},{160,192},{192,224},{224... | collective-permute-start | bytes 1572872 | tf_op jit(solution)/shard_map/ppermute | solution.py:18
  203.5 13.3 %collective-permute-start.11 = (bf16[512,512]{1,0:T(8,128)(2,1)S(1)}, bf16[512,512]{1,0:T(8,128)(2,1)S(1)}, u32[]{:S(2)}, u32[]{:S(2)}) collective-permute-start(bf16[512,512]{1,0:T(8,128)(2,1)S(1)} %collective-permute-done.10), channel_id=1, source_target_pairs={{0,32},{32,64},{64,96},{96,128},{128,160},{160,192},{192,224},{224... | collective-permute-start | bytes 1572872 | tf_op jit(solution)/shard_map/ppermute | solution.py:18
  216.8 12.4 %collective-permute-start.12 = (bf16[512,512]{1,0:T(8,128)(2,1)S(1)}, bf16[512,512]{1,0:T(8,128)(2,1)S(1)}, u32[]{:S(2)}, u32[]{:S(2)}) collective-permute-start(bf16[512,512]{1,0:T(8,128)(2,1)S(1)} %collective-permute-done.11), channel_id=1, source_target_pairs={{0,32},{32,64},{64,96},{96,128},{128,160},{160,192},{192,224},{224... | collective-permute-start | bytes 1572872 | tf_op jit(solution)/shard_map/ppermute | solution.py:18
  229.2 10.4 %collective-permute-start.13 = (bf16[512,512]{1,0:T(8,128)(2,1)S(1)}, bf16[512,512]{1,0:T(8,128)(2,1)S(1)}, u32[]{:S(2)}, u32[]{:S(2)}) collective-permute-start(bf16[512,512]{1,0:T(8,128)(2,1)S(1)} %collective-permute-done.12), channel_id=1, source_target_pairs={{0,32},{32,64},{64,96},{96,128},{128,160},{160,192},{192,224},{224... | collective-permute-start | bytes 1572872 | tf_op jit(solution)/shard_map/ppermute | solution.py:18
Sparse Core Ops, SparseCore 0:
  9.1 65.5 all-gather.2
  142.5 58.5 all-gather.4
